TPU v7x, 512 devices: a whole 4x8x8 slice. The times are simulated.
512 devices in a mesh: lat: 128 (over x, z_lo, y), chan: 4 (over z_hi, core).
Axes of the slice: x: 4, y: 8, z: 8 (z_hi: 2, z_lo: 4; z = z_hi * 4 + z_lo), core: 2. Of those that a mesh axis runs over, the one named last changes fastest.
Arguments:
- field: bfloat16 [640, 642, 544], P('lat', None, 'chan'), may hold values from -6 to 6
- cotangent: bfloat16 [640, 642, 1024], P('lat'), may hold values from -24 to 24
- weight: bfloat16 [544, 1024], P('chan'), may hold values from -0.25 to 0.25
- lon_counts: int32 [640], P('lat'), may hold values from 20 to 5136, as said below
- point_mask: int32 [640, 5136], P('lat', 'chan'), may hold values 0 or 1
Outputs:
- field_grad: bfloat16 [640, 642, 544], P('lat', None, 'chan')
- weight_grad: float32 [1024, 544], P('lat', 'chan')
Inputs may be any that keep to these rules, and one draw needn't show every extreme that they name: `lon_counts`: number of longitudes in use in a row; points from there to the end of the row are padding.
All inputs are finite; a program needn't handle non-finite values. No bound on the sum of `point_mask` on one device may be relied on, other than what follows from the above.
Results may differ from a plain program's by a relative error of at most 0.001.
Values sent between devices are 32-bit elements; how exact they have to be, the bound alone decides.
A program may use at most 64 MiB of HBM per device.

v0:
```python
import functools

import jax
import jax.numpy as jnp
from jax import lax
from jax.sharding import Mesh
from jax.sharding import PartitionSpec as P

P_SIZE = 8
LAT = ("lat_0", "lat_1", "lat_2")


def joined_along(parts, dim):
    dims = list(parts.shape[1:])
    dims[dim] *= parts.shape[0]
    return jnp.moveaxis(parts, 0, dim).reshape(dims)


def from_everyone(x, axis):
    size = lax.axis_size(axis)
    return lax.all_to_all(jnp.broadcast_to(x[None], (size, *x.shape)), axis, 0, 0, tiled=True)


def gather_directly(x, axis, dim):
    return joined_along(from_everyone(x, axis), dim)


def by_axis(x, axes):
    return functools.reduce(lax.psum, axes, x)


def cut_along(x, dim, size):
    before, after = (x.shape[:dim], x.shape[dim + 1 :])
    return jnp.moveaxis(x.reshape(*before, size, -1, *after), dim, 0)


def sum_at_owner(x, axis, dim):
    size = lax.axis_size(axis)
    parts = lax.all_to_all(cut_along(x, dim, size), axis, 0, 0, tiled=True)
    return jnp.sum(parts, axis=0)


def sum_by_axis(x, axes, dim):
    far, near = axes
    parts = cut_along(x, dim, lax.axis_size(far))
    nearer = sum_at_owner(parts, near, dim + 1)
    arrived = lax.all_to_all(nearer, far, split_axis=0, concat_axis=0, tiled=True)
    return arrived.sum(axis=0)


def local(field, cotangent, weight, lon_counts, point_mask):
    row_count, patch_count, features = field.shape
    channels = features // P_SIZE
    full_mask = gather_directly(point_mask, "chan", 1)
    positions = lax.broadcasted_iota(jnp.int32, full_mask.shape, 1)
    valid = jnp.where(positions < lon_counts[:, None], full_mask, 0)
    total = by_axis(jnp.sum(valid), LAT)
    scale = lax.rsqrt(jnp.maximum(total.astype(jnp.float32), 1.0))
    point_valid = valid.reshape(row_count, patch_count, 1, P_SIZE)
    masked = (
        field.reshape(row_count, patch_count, channels, P_SIZE) * point_valid.astype(jnp.bfloat16)
    ).reshape(row_count, patch_count, features)
    outcome = lax.dot_general(
        cotangent, weight, (((2,), (1,)), ((), ())), preferred_element_type=jnp.float32
    )
    field_grad = (
        (
            outcome.reshape(row_count, patch_count, channels, P_SIZE)
            * point_valid.astype(jnp.float32)
        )
        .reshape(row_count, patch_count, features)
        .astype(jnp.bfloat16)
    )
    summed = lax.dot_general(
        cotangent, masked, (((0, 1), (0, 1)), ((), ())), preferred_element_type=jnp.float32
    )
    weight_grad = sum_by_axis(summed * scale, ("lat_0", ("lat_1", "lat_2")), 0)
    return (field_grad, weight_grad)


def solution(mesh):
    split = Mesh(
        mesh.devices.reshape(4, 4, 8, mesh.shape["chan"]), ("lat_0", "lat_1", "lat_2", "chan")
    )
    in_specs = (P(LAT, None, "chan"), P(LAT, None, None), P("chan", None), P(LAT), P(LAT, "chan"))
    out_specs = (P(LAT, None, "chan"), P(LAT, "chan"))
    return jax.shard_map(local, mesh=split, in_specs=in_specs, out_specs=out_specs, check_vma=False)
```

profile of v0, /device:TPU:10, one launch (start us, length us, event | category | flops | bytes accessed | tf_op | source)
XLA Modules:
  0.0 102.9 jit_solution(7117397630759669773)
XLA Ops:
  0.6 0.0 copy-start
  0.6 1.5 %broadcast_in_dim.13 = s32[4,5,1284]{2,1,0:T(8,128)} broadcast(s32[5,1284]{1,0:T(8,128)} %param.9), dimensions={1,2} | broadcast | bytes 128400 | tf_op jit(solution)/shard_map/broadcast_in_dim | solution.py:21
  2.2 10.3 %all-to-all-start = ((s32[4,5,1284]{2,1,0:T(8,128)}), s32[4,5,1284]{2,1,0:T(8,128)S(1)}, u32[]{:S(2)}, u32[]{:S(2)}) async-start(s32[4,5,1284]{2,1,0:T(8,128)} %broadcast_in_dim.13), calls=%async_computation | async-start | bytes 360448 | tf_op jit(solution)/shard_map/all_to_all | solution.py:21
  12.4 11.0 %all-to-all-done = s32[4,5,1284]{2,1,0:T(8,128)S(1)} async-done(((s32[4,5,1284]{2,1,0:T(8,128)}), s32[4,5,1284]{2,1,0:T(8,128)S(1)}, u32[]{:S(2)}, u32[]{:S(2)}) %all-to-all-start) | async-done | bytes 102752 | tf_op jit(solution)/shard_map/all_to_all | solution.py:21
  23.4 1.4 %select_reduce_fusion = s32[]{:T(128)} fusion(s32[4,1284]{1,0:T(4,128)S(1)} %multiply_add_fusion.1, s32[5]{0:T(128)} %param.8, s32[4,5,1284]{2,1,0:T(8,128)S(1)} %all-to-all-done), kind=kLoop, calls=%fused_computation.8 | loop fusion | flops 77039 | bytes 123288 | tf_op jit(solution)/shard_map/reduce_sum | solution.py:57
  24.8 8.6 %psum.21 = s32[]{:T(128)} all-reduce(s32[]{:T(128)} %select_reduce_fusion), channel_id=1, replica_groups=mesh['lat_0'=4,'lat_1'=4,'lat_2'=8,'chan'=4] {'lat_0'}, use_global_device_ids=true, to_apply=%region_1.2 | all-reduce | flops 1 | bytes 8 | tf_op jit(solution)/shard_map/psum | solution.py:29
  33.4 8.8 %psum.22 = s32[]{:T(128)} all-reduce(s32[]{:T(128)} %psum.21), channel_id=1, replica_groups=mesh['lat_0'=4,'lat_1'=4,'lat_2'=8,'chan'=4] {'lat_1'}, use_global_device_ids=true, to_apply=%region_2.3 | all-reduce | flops 1 | bytes 8 | tf_op jit(solution)/shard_map/psum | solution.py:29
  42.2 13.8 %psum.23 = s32[]{:T(128)} all-reduce(s32[]{:T(128)} %psum.22), channel_id=1, replica_groups=mesh['lat_0'=4,'lat_1'=4,'lat_2'=8,'chan'=4] {'lat_2'}, use_global_device_ids=true, to_apply=%region_3.4 | all-reduce | flops 1 | bytes 8 | tf_op jit(solution)/shard_map/psum | solution.py:29
  56.8 0.7 reshape.69
  57.5 0.5 copy.21
  58.1 0.7 fusion.5
  58.8 4.5 %fusion.2 = f32[1024,136]{0,1:T(8,128)S(1)} fusion(bf16[5,642,1024]{2,1,0:T(8,128)(2,1)} %param.6, bf16[5,642,136]{1,2,0:T(8,128)(2,1)} %param.5, bf16[5,642,8]{1,2,0:T(8,128)(2,1)S(1)} %get-tuple-element.2, f32[]{:T(128)S(6)} %rsqrt.3), kind=kOutput, calls=%fused_computation.4 | convolution fusion | flops 894650688 | bytes 8055620 | tf_op jit(solution)/shard_map/dot_general | solution.py:74
  63.3 0.3 copy.22
  63.6 0.1 copy.23
  63.8 27.2 %all_to_all.15 = f32[32,4,8,136]{3,2,1,0:T(8,128)S(1)} all-to-all(f32[32,4,8,136]{3,2,1,0:T(8,128)S(1)} %copy.23), channel_id=1, replica_groups=mesh['lat_0'=4,'lat_1'=4,'lat_2'=8,'chan'=4] {'lat_1','lat_2'}, dimensions={0} | all-to-all | bytes 1114112 | tf_op jit(solution)/shard_map/all_to_all | solution.py:39
  91.0 0.7 reduce_sum.28
  91.6 4.7 %all-to-all-start.2 = ((f32[4,8,136]{2,1,0:T(8,128)}), f32[4,8,136]{2,1,0:T(8,128)S(1)}, u32[]{:S(2)}, u32[]{:S(2)}) async-start(f32[4,8,136]{2,1,0:T(8,128)} %reduce_sum.28), calls=%async_computation.2 | async-start | bytes 65536 | tf_op jit(solution)/shard_map/all_to_all | solution.py:47
  96.3 0.0 copy-done
  96.3 6.0 %fusion = bf16[5,642,136]{1,2,0:T(8,128)(2,1)} fusion(bf16[5,642,1024]{2,1,0:T(8,128)(2,1)} %param.6, f32[5,642,8]{1,2,0:T(8,128)S(1)} %get-tuple-element.3, bf16[136,1024]{1,0:T(8,128)(2,1)S(1)} %copy-done), kind=kOutput, calls=%fused_computation.1 | convolution fusion | flops 894947968 | bytes 7828448 | tf_op jit(solution)/shard_map/dot_general | solution.py:63
  102.3 0.0 all-to-all-done.2
  102.3 0.6 reduce_sum.29
  (3 shorter events, 0.0 us)
Async XLA Ops:
  0.6 95.7 %copy-start = (bf16[136,1024]{1,0:T(8,128)(2,1)S(1)}, bf16[136,1024]{1,0:T(8,128)(2,1)}, u32[]{:S(2)}) copy-start(bf16[136,1024]{1,0:T(8,128)(2,1)} %param.7) | copy-start | bytes 835588
  2.2 21.2 %all-to-all-start = ((s32[4,5,1284]{2,1,0:T(8,128)}), s32[4,5,1284]{2,1,0:T(8,128)S(1)}, u32[]{:S(2)}, u32[]{:S(2)}) async-start(s32[4,5,1284]{2,1,0:T(8,128)} %broadcast_in_dim.13), calls=%async_computation | async-start | bytes 360448 | tf_op jit(solution)/shard_map/all_to_all | solution.py:21
  91.6 10.7 %all-to-all-start.2 = ((f32[4,8,136]{2,1,0:T(8,128)}), f32[4,8,136]{2,1,0:T(8,128)S(1)}, u32[]{:S(2)}, u32[]{:S(2)}) async-start(f32[4,8,136]{2,1,0:T(8,128)} %reduce_sum.28), calls=%async_computation.2 | async-start | bytes 65536 | tf_op jit(solution)/shard_map/all_to_all | solution.py:47
where the time goes:
time: 103 us
  blocking collectives  58.4 us (57%)
  starting transfers between devices  14.9 us (14%)
  waiting for transfers between devices  11 us (11%)
  matrix products  10.5 us (10%)
  other arithmetic  3.46 us (3%)
  local copies, waits for them, and re-layouts  3.29 us (3%)
  between operations  1.38 us (1%)
    psum x3, blocking collectives, by_axis(): return functools.reduce(lax.psum, axes, x)  31.2 us
    all_to_all x1, blocking collectives, sum_at_owner(): parts = lax.all_to_all(cut_along(x, dim, size), axis, 0, 0, tiled=True)  27.2 us
    all_to_all x1, waiting for transfers between devices, from_everyone(): lax.all_to_all(jnp.broadcast_to(x[None], (size, *x.shape)), axis, 0, 0, t...  11 us
    all_to_all x1, starting transfers between devices, from_everyone(): lax.all_to_all(jnp.broadcast_to(x[None], (size, *x.shape)), axis, 0, 0, t...  10.3 us
    dot_general x1, matrix products, local(): lax.dot_general(cotangent, weight, (((2,), (1,)), ((), ())), preferred_el...  6 us
    all_to_all x1, starting transfers between devices, sum_by_axis(): lax.all_to_all(nearer, far, split_axis=0, concat_axis=0, tiled=True)  4.66 us
    dot_general x1, matrix products, local(): lax.dot_general(cotangent, masked, (((0, 1), (0, 1)), ((), ())), preferre...  4.45 us
  transfers between devices with their start and end apart: 2, of which 1 were waited for; matrix products, arithmetic and copies ran while one was open for 6% of the time, Pallas kernels for 0%

commit v1 on v0

v1 whole, which is shorter than its diff:
```python
import functools

import jax
import jax.numpy as jnp
from jax import lax
from jax.experimental import pallas as pl
from jax.experimental.pallas import tpu as pltpu
from jax.sharding import Mesh
from jax.sharding import PartitionSpec as P

MESH = pl.DeviceIdType.MESH
AXES = ("x", "z", "y", "zh", "core")
LAT = ("x", "z", "y")
CHAN = ("zh", "core")
F32 = jnp.float32
BF16 = jnp.bfloat16

ROWS = 5
PATCHES = 642
F = 136
E = 1024
PART = 1284
BASES = (0, 128, 256, 384)
WIDTHS = (256, 256, 256, 384)
LANES = 768
Z_ROWS = 72


def iota(shape, dim):
    return lax.broadcasted_iota(jnp.int32, shape, dim)


def kernel(
    ft_hbm, cot_hbm, w_hbm, counts, mask_hbm,
    fg_hbm, wg_ref,
    ft, cot, w, masks, pick, valid, prod, fm,
    x_send, x_recv, z_send, z_recv, y_send, y_recv,
    cot_sem, ft_sem, w_sem, mask_sem, out_sem,
    m_ssem, m_rsem, x_ssem, x_rsem, z_ssem, z_rsem, y_ssem, y_rsem,
):
    x, z, y = (lax.axis_index(a) for a in LAT)
    zh, core = (lax.axis_index(a) for a in CHAN)
    me = zh * 2 + core

    barrier = pltpu.get_barrier_semaphore()

    def greet(device):
        pl.semaphore_signal(barrier, inc=1, device_id=device, device_id_type=MESH)

    for d in range(1, 4):
        greet({"zh": zh ^ (d // 2), "core": core ^ (d % 2)})
    for d in range(1, 4):
        greet({"x": (x + d) % 4})
    for d in range(1, 4):
        greet({"z": (z + d) % 4})
    for d in range(1, 8):
        greet({"y": (y + d) % 8})

    own_mask = pltpu.make_async_copy(mask_hbm, masks.at[me], mask_sem)
    own_mask.start()
    w_copy = pltpu.make_async_copy(w_hbm, w, w_sem)
    w_copy.start()
    cot_copies = [pltpu.make_async_copy(cot_hbm.at[r], cot.at[r], cot_sem.at[r]) for r in range(ROWS)]
    ft_copies = [pltpu.make_async_copy(ft_hbm.at[r], ft.at[r], ft_sem.at[r]) for r in range(ROWS)]
    for c in cot_copies + ft_copies:
        c.start()

    own_mask.wait()
    pl.semaphore_wait(barrier, 16)

    mask_copies = []
    for d in (3, 2, 1):
        copy = pltpu.make_async_remote_copy(
            src_ref=masks.at[me],
            dst_ref=masks.at[me],
            send_sem=m_ssem.at[d - 1],
            recv_sem=m_rsem.at[d - 1],
            device_id={"zh": zh ^ (d // 2), "core": core ^ (d % 2)},
            device_id_type=MESH,
        )
        copy.start()
        mask_copies.append(copy)

    for j in range(4):
        at = (iota((PART, WIDTHS[j]), 0) + PART * j) // 8 - BASES[j]
        hit = at == iota((PART, WIDTHS[j]), 1)
        pick[j, :, : WIDTHS[j]] = jnp.where(hit, 1.0, 0.0).astype(BF16)
    valid[...] = jnp.zeros_like(valid)

    w_copy.wait()
    for r in range(ROWS):
        cot_copies[r].wait()
        for p in range(0, PATCHES, 256):
            n = min(256, PATCHES - p)
            prod[r, :, p : p + n] = lax.dot_general(
                w[...], cot[r, p : p + n, :], (((1,), (1,)), ((), ())), preferred_element_type=F32
            ).astype(BF16)

    for copy in mask_copies:
        copy.wait_recv()
    for c in ft_copies:
        c.wait()

    for j in range(4):
        spot = iota((8, PART), 1) + PART * j
        phase = spot % 8 == iota((8, PART), 0)
        rows = []
        for r in range(ROWS):
            keep = jnp.logical_and(phase, spot < counts[r])
            line = jnp.broadcast_to(masks[j, r : r + 1, :], (8, PART)).astype(F32)
            rows.append(jnp.where(keep, line, 0.0))
        spread = jnp.concatenate(rows, axis=0).astype(BF16)
        placed = jnp.dot(spread, pick[j, :, : WIDTHS[j]], preferred_element_type=F32)
        for r in range(ROWS):
            valid[r, :, BASES[j] : BASES[j] + WIDTHS[j]] += placed[8 * r : 8 * r + 8]

    count = jnp.zeros((8, 128), F32)
    for r in range(ROWS):
        v = valid[r]
        for t in range(LANES // 128):
            count = count + v[:, 128 * t : 128 * t + 128]
        v = v[:, :PATCHES]
        v16 = jnp.concatenate([v, v], axis=0).astype(BF16)
        for c in range(0, 128, 16):
            fm[r, c : c + 16, :] = ft[r, c : c + 16, :] * v16
        fm[r, 128:136, :] = ft[r, 128:136, :] * v16[:8]

    x_copies = []
    for d in (2, 1, 3, 0):
        to = (x + d) % 4
        lanes = pl.ds(pl.multiple_of(to * 256, 256), 256)
        acc = jnp.dot(fm[0], cot[0, :, lanes], preferred_element_type=F32)
        for r in range(1, ROWS):
            acc = acc + jnp.dot(fm[r], cot[r, :, lanes], preferred_element_type=F32)
        x_send[d, :F, :] = acc
        x_send[d, F : F + 8, :128] = count
        x_send[d, F : F + 8, 128:] = count
        if d:
            copy = pltpu.make_async_remote_copy(
                src_ref=x_send.at[d],
                dst_ref=x_recv.at[d - 1],
                send_sem=x_ssem.at[d - 1],
                recv_sem=x_rsem.at[d - 1],
                device_id={"x": to},
                device_id_type=MESH,
            )
            copy.start()
            x_copies.append(copy)

    out_copies = []
    for r in range(ROWS):
        v = valid[r][:, :PATCHES]
        v16 = jnp.concatenate([v, v], axis=0).astype(BF16)
        for c in range(0, 128, 16):
            prod[r, c : c + 16, :] = prod[r, c : c + 16, :] * v16
        prod[r, 128:136, :] = prod[r, 128:136, :] * v16[:8]
        copy = pltpu.make_async_copy(prod.at[r], fg_hbm.at[r], out_sem.at[r])
        copy.start()
        out_copies.append(copy)

    for copy in x_copies:
        copy.wait_recv()
    total = x_send[0] + x_recv[0] + x_recv[1] + x_recv[2]
    turned = jnp.transpose(total[:128, :])
    rest = total[128:F, :]
    counted = total[F : F + 8, :128] + pltpu.roll(total[F : F + 8, :128], 64, 1)
    half = iota((8, 128), 1) // 64
    for to in range(4):
        z_send[to, :64, :] = turned[64 * to : 64 * to + 64, :]
        tile = rest[:, 128 * (to // 2) : 128 * (to // 2) + 128]
        z_send[to, 64:72, :] = jnp.where(half == to % 2, tile, counted)

    z_copies = []
    for d in (2, 1, 3):
        to = (z + d) % 4
        copy = pltpu.make_async_remote_copy(
            src_ref=z_send.at[to],
            dst_ref=z_recv.at[d - 1],
            send_sem=z_ssem.at[d - 1],
            recv_sem=z_rsem.at[d - 1],
            device_id={"z": to},
            device_id_type=MESH,
        )
        copy.start()
        z_copies.append(copy)
    for copy in z_copies:
        copy.wait_recv()
    nearer = z_send[z] + z_recv[0] + z_recv[1] + z_recv[2]
    for to in range(8):
        y_send[to, :8, :] = nearer[8 * to : 8 * to + 8, :]
        y_send[to, 8:16, :] = nearer[64:72, :]

    y_copies = []
    for d in (4, 3, 5, 2, 6, 1, 7):
        to = (y + d) % 8
        copy = pltpu.make_async_remote_copy(
            src_ref=y_send.at[to],
            dst_ref=y_recv.at[d - 1],
            send_sem=y_ssem.at[d - 1],
            recv_sem=y_rsem.at[d - 1],
            device_id={"y": to},
            device_id_type=MESH,
        )
        copy.start()
        y_copies.append(copy)
    for copy in y_copies:
        copy.wait_recv()
    last = y_send[y]
    for d in range(7):
        last = last + y_recv[d]
    tile = last[8:16, :]
    other = jnp.where(half == z % 2, 0.0, tile)
    points = jnp.sum(jnp.sum(other, axis=1, keepdims=True), axis=0, keepdims=True)
    scale = lax.rsqrt(jnp.maximum(points, 1.0))
    wg_ref[:, :128] = last[:8, :] * scale
    moved = pltpu.roll(tile, (128 - ((z % 2) * 64 + y * 8)) % 128, 1)
    wg_ref[:, 128:136] = jnp.transpose(moved)[:8, :] * scale

    for copy in mask_copies + x_copies + z_copies + y_copies:
        copy.wait_send()
    for copy in out_copies:
        copy.wait()


def local(field, cotangent, weight, lon_counts, point_mask):
    ft = jnp.transpose(field, (0, 2, 1))
    any_space = pl.BlockSpec(memory_space=pl.ANY)
    dma = pltpu.SemaphoreType.DMA
    fg, wg = pl.pallas_call(
        kernel,
        out_shape=(
            jax.ShapeDtypeStruct((ROWS, F, PATCHES), BF16),
            jax.ShapeDtypeStruct((8, F), F32),
        ),
        in_specs=[any_space, any_space, any_space, pl.BlockSpec(memory_space=pltpu.SMEM), any_space],
        out_specs=(any_space, pl.BlockSpec(memory_space=pltpu.VMEM)),
        scratch_shapes=[
            pltpu.VMEM((ROWS, F, PATCHES), BF16),
            pltpu.VMEM((ROWS, PATCHES, E), BF16),
            pltpu.VMEM((F, E), BF16),
            pltpu.VMEM((4, ROWS, PART), jnp.int32),
            pltpu.VMEM((4, PART, 384), BF16),
            pltpu.VMEM((ROWS, 8, LANES), F32),
            pltpu.VMEM((ROWS, F, PATCHES), BF16),
            pltpu.VMEM((ROWS, F, PATCHES), BF16),
            pltpu.VMEM((4, F + 8, 256), F32),
            pltpu.VMEM((3, F + 8, 256), F32),
            pltpu.VMEM((4, Z_ROWS, 128), F32),
            pltpu.VMEM((3, Z_ROWS, 128), F32),
            pltpu.VMEM((8, 16, 128), F32),
            pltpu.VMEM((7, 16, 128), F32),
            dma((ROWS,)), dma((ROWS,)), dma, dma, dma((ROWS,)),
            dma((3,)), dma((3,)), dma((3,)), dma((3,)), dma((3,)), dma((3,)), dma((7,)), dma((7,)),
        ],
        compiler_params=pltpu.CompilerParams(
            collective_id=0, has_side_effects=True, vmem_limit_bytes=60 * 1024 * 1024
        ),
        name="backward",
    )(ft, cotangent, weight, lon_counts, point_mask)
    return jnp.transpose(fg, (0, 2, 1)), wg


def solution(mesh):
    split = Mesh(mesh.devices.reshape(4, 4, 8, 2, 2), AXES)
    in_specs = (P(LAT, None, CHAN), P(LAT, None, None), P(CHAN, None), P(LAT), P(LAT, CHAN))
    out_specs = (P(LAT, None, CHAN), P(LAT, CHAN))
    return jax.shard_map(local, mesh=split, in_specs=in_specs, out_specs=out_specs, check_vma=False)
```

time: 103 us -> 48.3 us (0.47)
  the two profiles are of different devices: /device:TPU:10 before, /device:TPU:1 now
where the time goes in v1:
time: 48.3 us; the launch traced here: 48.1 us
  Pallas kernels  43.9 us (91%)
  local copies, waits for them, and re-layouts  3.55 us (7%)
  between operations  0.64 us (1%)
    pallas_call x1, Pallas kernels, local(): pl.pallas_call(kernel, out_shape=(jax.ShapeDtypeStruct((ROWS, F, PATCHES)...  43.9 us
    unnamed x2, local copies, waits for them, and re-layouts  3.55 us

profile of v1, /device:TPU:1, one launch (start us, length us, event | category | flops | bytes accessed | tf_op | source)
XLA Modules:
  0.0 48.1 jit_solution(10635715790400413208)
XLA Ops:
  0.6 43.9 %backward.1 = (bf16[5,136,642]{2,1,0:T(8,128)(2,1)}, f32[8,136]{1,0:T(8,128)}) custom-call(bf16[5,136,642]{2,1,0:T(8,128)(2,1)} %bitcast.2, bf16[5,642,1024]{2,1,0:T(8,128)(2,1)} %cot_hbm.1, bf16[136,1024]{1,0:T(8,128)(2,1)} %w_hbm.1, s32[5]{0:T(128)} %counts.1, s32[5,1284]{1,0:T(8,128)} %mask_hbm.1), custom_call_target="tpu_custom_call" | custom-call | tf_op jit(solution)/shard_map/backward/pallas_call | solution.py:229
  44.5 2.3 %copy.9 = bf16[5,642,136]{1,2,0:T(8,128)(2,1)} copy(bf16[5,642,136]{1,2,0:T(8,128)(2,1)} %bitcast.3) | data formatting | bytes 1746240
  46.8 1.3 %copy.10 = f32[8,136]{1,0:T(8,128)} copy(f32[8,136]{1,0:T(8,128)} %get-tuple-element.9) | data formatting | bytes 8704

commit v2 on v1

v2 whole, which is shorter than its diff:
```python
import functools

import jax
import jax.numpy as jnp
from jax import lax
from jax.experimental import pallas as pl
from jax.experimental.pallas import tpu as pltpu
from jax.sharding import Mesh
from jax.sharding import PartitionSpec as P

MESH = pl.DeviceIdType.MESH
AXES = ("x", "z", "y", "zh", "core")
LAT = ("x", "z", "y")
CHAN = ("zh", "core")
F32 = jnp.float32
BF16 = jnp.bfloat16

ROWS = 5
PATCHES = 642
F = 136
E = 1024
PART = 1284
WIDTH = 384
LANES = 768
Z_ROWS = 72


def iota(shape, dim):
    return lax.broadcasted_iota(jnp.int32, shape, dim)


def kernel(
    ft_hbm, cot_hbm, w_hbm, counts_hbm, mask_hbm,
    fg_ref, wg_ref,
    ft, cot, w, counts, masks, pick, valid, fm,
    x_send, x_recv, c_send, c_recv, z_send, z_recv, y_send, y_recv,
    cot_sem, ft_sem, w_sem, counts_sem, mask_sem,
    m_ssem, m_rsem, x_ssem, x_rsem, c_ssem, c_rsem, z_ssem, z_rsem, y_ssem, y_rsem,
):
    x, z, y = (lax.axis_index(a) for a in LAT)
    zh, core = (lax.axis_index(a) for a in CHAN)
    me = zh * 2 + core
    mate = zh * 2 + 1 - core
    far = (1 - zh) * 2 + core
    far_mate = (1 - zh) * 2 + 1 - core

    own_mask = pltpu.make_async_copy(mask_hbm, masks.at[me], mask_sem)
    own_mask.start()
    own_counts = pltpu.make_async_copy(counts_hbm, counts, counts_sem)
    own_counts.start()

    barrier = pltpu.get_barrier_semaphore()

    def greet(device):
        pl.semaphore_signal(barrier, inc=1, device_id=device, device_id_type=MESH)

    greet({"zh": 1 - zh})
    greet({"core": 1 - core})
    for d in (1, 2, 3):
        greet({"x": (x + d) % 4})
        greet({"z": (z + d) % 4})
    for d in range(1, 8):
        greet({"y": (y + d) % 8})

    shards = (me, mate, far, far_mate)
    for i, j in enumerate(shards):
        at = ((iota((PART, WIDTH), 0) + PART * j) >> 3) - 128 * j
        hit = at == iota((PART, WIDTH), 1)
        pick[i] = jnp.where(hit, 1.0, 0.0).astype(BF16)
    valid[...] = jnp.zeros_like(valid)

    own_mask.wait()
    own_counts.wait()
    w_copy = pltpu.make_async_copy(w_hbm, w, w_sem)
    cot_copies = [pltpu.make_async_copy(cot_hbm.at[r], cot.at[r], cot_sem.at[r]) for r in range(ROWS)]
    ft_copies = [pltpu.make_async_copy(ft_hbm.at[r], ft.at[r], ft_sem.at[r]) for r in range(ROWS)]

    def mask_to(i, shard, device):
        return pltpu.make_async_remote_copy(
            src_ref=masks.at[shard],
            dst_ref=masks.at[shard],
            send_sem=m_ssem.at[i],
            recv_sem=m_rsem.at[i],
            device_id=device,
            device_id_type=MESH,
        )

    def place(i):
        j = shards[i]
        spot = iota((8, PART), 1) + PART * j
        phase = (spot & 7) == iota((8, PART), 0)
        rows = []
        for r in range(ROWS):
            keep = jnp.logical_and(phase, spot < counts[r])
            line = jnp.broadcast_to(masks[j, r : r + 1, :], (8, PART)).astype(F32)
            rows.append(jnp.where(keep, line, 0.0))
        spread = jnp.concatenate(rows, axis=0).astype(BF16)
        placed = jnp.dot(spread, pick[i], preferred_element_type=F32)
        lanes = pl.ds(pl.multiple_of(j * 128, 128), WIDTH)
        for r in range(ROWS):
            valid[r, :, lanes] += placed[8 * r : 8 * r + 8]

    for c in ft_copies + cot_copies + [w_copy]:
        c.start()
    pl.semaphore_wait(barrier, 15)
    to_far = mask_to(0, me, {"zh": 1 - zh})
    to_far.start()
    to_mate = mask_to(1, me, {"core": 1 - core})
    to_mate.start()
    place(0)
    to_mate.wait_recv()
    place(1)
    to_far.wait_recv()
    relay = mask_to(2, far, {"core": 1 - core})
    relay.start()
    place(2)
    for c in ft_copies:
        c.wait()
    relay.wait_recv()
    place(3)

    count = jnp.zeros((8, 128), F32)
    for r in range(ROWS):
        v = valid[r]
        for t in range(LANES // 128):
            count = count + v[:, 128 * t : 128 * t + 128]
        v = v[:, :PATCHES]
        v16 = jnp.concatenate([v, v], axis=0).astype(BF16)
        for c in range(0, 128, 16):
            fm[r, c : c + 16, :] = ft[r, c : c + 16, :] * v16
        fm[r, 128:136, :] = ft[r, 128:136, :] * v16[:8]
    c_send[...] = count
    for c in cot_copies:
        c.wait()

    x_copies = []
    for d in (2, 1, 3, 0):
        to = (x + d) % 4
        lanes = pl.ds(pl.multiple_of(to * 256, 256), 256)
        acc = jnp.dot(fm[0], cot[0, :, lanes], preferred_element_type=F32)
        for r in range(1, ROWS):
            acc = acc + jnp.dot(fm[r], cot[r, :, lanes], preferred_element_type=F32)
        x_send[d] = acc
        if d:
            for source, target, ssem, rsem in (
                (x_send.at[d], x_recv.at[d - 1], x_ssem, x_rsem),
                (c_send, c_recv.at[d - 1], c_ssem, c_rsem),
            ):
                copy = pltpu.make_async_remote_copy(
                    src_ref=source,
                    dst_ref=target,
                    send_sem=ssem.at[d - 1],
                    recv_sem=rsem.at[d - 1],
                    device_id={"x": to},
                    device_id_type=MESH,
                )
                copy.start()
                x_copies.append(copy)

    w_copy.wait()
    for r in range(ROWS):
        v = valid[r][:, :PATCHES]
        v16 = jnp.concatenate([v] * 17, axis=0)
        for p in range(0, PATCHES, 256):
            n = min(256, PATCHES - p)
            product = lax.dot_general(
                w[...], cot[r, p : p + n, :], (((1,), (1,)), ((), ())), preferred_element_type=F32
            )
            fg_ref[r, :, p : p + n] = (product * v16[:, p : p + n]).astype(BF16)

    for copy in x_copies:
        copy.wait_recv()
    total = x_send[0] + x_recv[0] + x_recv[1] + x_recv[2]
    turned = jnp.transpose(total[:128, :])
    rest = total[128:F, :]
    counted = c_send[...] + c_recv[0] + c_recv[1] + c_recv[2]
    counted = counted + pltpu.roll(counted, 64, 1)
    half = iota((8, 128), 1) // 64
    for to in range(4):
        z_send[to, :64, :] = turned[64 * to : 64 * to + 64, :]
        tile = rest[:, 128 * (to // 2) : 128 * (to // 2) + 128]
        z_send[to, 64:72, :] = jnp.where(half == to % 2, tile, counted)

    z_copies = []
    for d in (2, 1, 3):
        to = (z + d) % 4
        copy = pltpu.make_async_remote_copy(
            src_ref=z_send.at[to],
            dst_ref=z_recv.at[d - 1],
            send_sem=z_ssem.at[d - 1],
            recv_sem=z_rsem.at[d - 1],
            device_id={"z": to},
            device_id_type=MESH,
        )
        copy.start()
        z_copies.append(copy)
    for copy in z_copies:
        copy.wait_recv()
    nearer = z_send[z] + z_recv[0] + z_recv[1] + z_recv[2]
    for to in range(8):
        y_send[to, :8, :] = nearer[8 * to : 8 * to + 8, :]
        y_send[to, 8:16, :] = nearer[64:72, :]

    y_copies = []
    for d in (4, 3, 5, 2, 6, 1, 7):
        to = (y + d) % 8
        copy = pltpu.make_async_remote_copy(
            src_ref=y_send.at[to],
            dst_ref=y_recv.at[d - 1],
            send_sem=y_ssem.at[d - 1],
            recv_sem=y_rsem.at[d - 1],
            device_id={"y": to},
            device_id_type=MESH,
        )
        copy.start()
        y_copies.append(copy)
    for copy in y_copies:
        copy.wait_recv()
    last = y_send[y]
    for d in range(7):
        last = last + y_recv[d]
    tile = last[8:16, :]
    other = jnp.where(half == z % 2, 0.0, tile)
    points = jnp.sum(jnp.sum(other, axis=1, keepdims=True), axis=0, keepdims=True)
    scale = lax.rsqrt(jnp.maximum(points, 1.0))
    wg_ref[:, :128] = last[:8, :] * scale
    moved = pltpu.roll(tile, (128 - ((z % 2) * 64 + y * 8)) % 128, 1)
    wg_ref[:, 128:136] = jnp.transpose(moved)[:8, :] * scale

    for copy in [to_far, to_mate, relay] + x_copies + z_copies + y_copies:
        copy.wait_send()


def local(field, cotangent, weight, lon_counts, point_mask):
    ft = jnp.transpose(field, (0, 2, 1))
    hbm = pl.BlockSpec(memory_space=pltpu.HBM)
    vmem = pl.BlockSpec(memory_space=pltpu.VMEM)
    dma = pltpu.SemaphoreType.DMA
    fg, wg = pl.pallas_call(
        kernel,
        out_shape=(pltpu.VMEM((ROWS, F, PATCHES), BF16), pltpu.VMEM((8, F), F32)),
        in_specs=[hbm] * 5,
        out_specs=(vmem, vmem),
        scratch_shapes=[
            pltpu.VMEM((ROWS, F, PATCHES), BF16),
            pltpu.VMEM((ROWS, PATCHES, E), BF16),
            pltpu.VMEM((F, E), BF16),
            pltpu.SMEM((ROWS,), jnp.int32),
            pltpu.VMEM((4, ROWS, PART), jnp.int32),
            pltpu.VMEM((4, PART, WIDTH), BF16),
            pltpu.VMEM((ROWS, 8, LANES), F32),
            pltpu.VMEM((ROWS, F, PATCHES), BF16),
            pltpu.VMEM((4, F, 256), F32),
            pltpu.VMEM((3, F, 256), F32),
            pltpu.VMEM((8, 128), F32),
            pltpu.VMEM((3, 8, 128), F32),
            pltpu.VMEM((4, Z_ROWS, 128), F32),
            pltpu.VMEM((3, Z_ROWS, 128), F32),
            pltpu.VMEM((8, 16, 128), F32),
            pltpu.VMEM((7, 16, 128), F32),
            dma((ROWS,)), dma((ROWS,)), dma, dma, dma,
            dma((3,)), dma((3,)), dma((3,)), dma((3,)), dma((3,)), dma((3,)),
            dma((3,)), dma((3,)), dma((7,)), dma((7,)),
        ],
        compiler_params=pltpu.CompilerParams(
            collective_id=0, has_side_effects=True, vmem_limit_bytes=40 * 1024 * 1024
        ),
        name="backward",
    )(*(pltpu.with_memory_space_constraint(v, pltpu.HBM) for v in (ft, cotangent, weight, lon_counts, point_mask)))
    return jnp.transpose(fg, (0, 2, 1)), wg


def solution(mesh):
    split = Mesh(mesh.devices.reshape(4, 4, 8, 2, 2), AXES)
    in_specs = (P(LAT, None, CHAN), P(LAT, None, None), P(CHAN, None), P(LAT), P(LAT, CHAN))
    out_specs = (P(LAT, None, CHAN), P(LAT, CHAN))
    return jax.shard_map(local, mesh=split, in_specs=in_specs, out_specs=out_specs, check_vma=False)
```

time: 48.3 us -> 42.2 us (0.87); the launches traced: 48.1 us -> 41.4 us
  Pallas kernels: 43.9 us -> 39.2 us
  local copies, waits for them, and re-layouts: 3.55 us -> 1.56 us
    pallas_call x1, Pallas kernels: 43.9 us -> 39.2 us  [local(): pl.pallas_call(kernel, out_shape=(pltpu.VMEM((ROWS, F, PATCHES), BF16), p...]
    unnamed x2, local copies, waits for them, and re-layouts: 3.55 us -> 1.56 us
where the time goes in v2:
time: 42.2 us; the launch traced here: 41.4 us
  Pallas kernels  39.2 us (93%)
  local copies, waits for them, and re-layouts  1.56 us (4%)
  between operations  0.64 us (2%)
    pallas_call x1, Pallas kernels, local(): pl.pallas_call(kernel, out_shape=(pltpu.VMEM((ROWS, F, PATCHES), BF16), p...  39.2 us
    unnamed x2, local copies, waits for them, and re-layouts  1.56 us

profile of v2, /device:TPU:1, one launch (start us, length us, event | category | flops | bytes accessed | tf_op | source)
XLA Modules:
  0.0 41.4 jit_solution(11385008315789210484)
XLA Ops:
  0.6 39.2 %backward.1 = (bf16[5,136,642]{2,1,0:T(8,128)(2,1)S(1)}, f32[8,136]{1,0:T(8,128)S(1)}) custom-call(bf16[5,136,642]{2,1,0:T(8,128)(2,1)} %bitcast.3, bf16[5,642,1024]{2,1,0:T(8,128)(2,1)} %cot_hbm.1, bf16[136,1024]{1,0:T(8,128)(2,1)} %w_hbm.1, s32[5]{0:T(128)} %counts_hbm.1, s32[5,1284]{1,0:T(8,128)} %mask_hbm.1), custom_call_target="tpu_custom_call" | custom-call | tf_op jit(solution)/shard_map/backward/pallas_call | solution.py:239
  39.9 1.0 %copy.9 = bf16[5,642,136]{1,2,0:T(8,128)(2,1)} copy(bf16[5,642,136]{1,2,0:T(8,128)(2,1)S(1)} %bitcast.2) | data formatting | bytes 1746240
  40.8 0.6 %copy.10 = f32[8,136]{1,0:T(8,128)} copy(f32[8,136]{1,0:T(8,128)S(1)} %get-tuple-element.7) | data formatting | bytes 8704

commit v3 on v2

--- a/solution.py
+++ b/solution.py
@@ -23,6 +23,7 @@
 WIDTH = 384
 LANES = 768
 Z_ROWS = 72
+TOP = 72
 
 
 def iota(shape, dim):
@@ -33,9 +34,9 @@
     ft_hbm, cot_hbm, w_hbm, counts_hbm, mask_hbm,
     fg_ref, wg_ref,
     ft, cot, w, counts, masks, pick, valid, fm,
-    x_send, x_recv, c_send, c_recv, z_send, z_recv, y_send, y_recv,
+    x_two, x_up, x_down, x_own, s_up, s_down, r_up, r_down, c_send, c_recv, z_send, z_recv, y_send, y_recv,
     cot_sem, ft_sem, w_sem, counts_sem, mask_sem,
-    m_ssem, m_rsem, x_ssem, x_rsem, c_ssem, c_rsem, z_ssem, z_rsem, y_ssem, y_rsem,
+    m_ssem, m_rsem, u_ssem, u_rsem, d_ssem, d_rsem, c_ssem, c_rsem, z_ssem, z_rsem, y_ssem, y_rsem,
 ):
     x, z, y = (lax.axis_index(a) for a in LAT)
     zh, core = (lax.axis_index(a) for a in CHAN)
@@ -130,32 +131,103 @@
             fm[r, c : c + 16, :] = ft[r, c : c + 16, :] * v16
         fm[r, 128:136, :] = ft[r, 128:136, :] * v16[:8]
     c_send[...] = count
+    c_copies = []
+    for d in (2, 1, 3):
+        copy = pltpu.make_async_remote_copy(
+            src_ref=c_send,
+            dst_ref=c_recv.at[d - 1],
+            send_sem=c_ssem.at[d - 1],
+            recv_sem=c_rsem.at[d - 1],
+            device_id={"x": (x + d) % 4},
+            device_id_type=MESH,
+        )
+        copy.start()
+        c_copies.append(copy)
     for c in cot_copies:
         c.wait()
 
-    x_copies = []
-    for d in (2, 1, 3, 0):
-        to = (x + d) % 4
+    top, low = pl.ds(0, TOP), pl.ds(TOP, F - TOP)
+    up, down = (x + 1) % 4, (x + 3) % 4
+
+    def block(to, ref):
         lanes = pl.ds(pl.multiple_of(to * 256, 256), 256)
         acc = jnp.dot(fm[0], cot[0, :, lanes], preferred_element_type=F32)
         for r in range(1, ROWS):
             acc = acc + jnp.dot(fm[r], cot[r, :, lanes], preferred_element_type=F32)
-        x_send[d] = acc
-        if d:
-            for source, target, ssem, rsem in (
-                (x_send.at[d], x_recv.at[d - 1], x_ssem, x_rsem),
-                (c_send, c_recv.at[d - 1], c_ssem, c_rsem),
-            ):
-                copy = pltpu.make_async_remote_copy(
-                    src_ref=source,
-                    dst_ref=target,
-                    send_sem=ssem.at[d - 1],
-                    recv_sem=rsem.at[d - 1],
-                    device_id={"x": to},
-                    device_id_type=MESH,
-                )
-                copy.start()
-                x_copies.append(copy)
+        ref[0] = acc[:, :128]
+        ref[1] = acc[:, 128:]
+
+    def x_copy(source, target, sems, i, to):
+        return pltpu.make_async_remote_copy(
+            src_ref=source,
+            dst_ref=target,
+            send_sem=sems[0].at[i],
+            recv_sem=sems[1].at[i],
+            device_id={"x": to},
+            device_id_type=MESH,
+        )
+
+    ups, downs = (u_ssem, u_rsem), (d_ssem, d_rsem)
+    first_up = [x_copy(x_two.at[h, top], s_up.at[h], ups, h, up) for h in range(2)]
+    first_down = [x_copy(x_two.at[h, low], s_down.at[h], downs, h, down) for h in range(2)]
+    plain_up = [x_copy(x_up.at[h, low], r_up.at[h, low], ups, 2 + h, up) for h in range(2)]
+    plain_down = [x_copy(x_down.at[h, top], r_down.at[h, top], downs, 2 + h, down) for h in range(2)]
+    sum_up = [x_copy(x_up.at[h, top], r_up.at[h, top], ups, 4 + h, up) for h in range(2)]
+    sum_down = [x_copy(x_down.at[h, low], r_down.at[h, low], downs, 4 + h, down) for h in range(2)]
+
+    block((x + 2) % 4, x_two)
+    for h in range(2):
+        first_up[h].start()
+        first_down[h].start()
+    block(up, x_up)
+    plain_up[0].start()
+    block(down, x_down)
+    plain_down[0].start()
+    block(x, x_own)
+    for h in range(2):
+        first_up[h].wait_recv()
+        x_up[h, top, :] += s_up[h]
+        sum_up[h].start()
+        first_down[h].wait_recv()
+        x_down[h, low, :] += s_down[h]
+        sum_down[h].start()
+        if h == 0:
+            plain_up[1].start()
+            plain_down[1].start()
+    for copy in c_copies:
+        copy.wait_recv()
+    counted = c_send[...] + c_recv[0] + c_recv[1] + c_recv[2]
+    counted = counted + pltpu.roll(counted, 64, 1)
+    half = iota((8, 128), 1) // 64
+
+    def z_copy(to):
+        return pltpu.make_async_remote_copy(
+            src_ref=z_send.at[to],
+            dst_ref=z_recv.at[z],
+            send_sem=z_ssem.at[to],
+            recv_sem=z_rsem.at[z],
+            device_id={"z": to},
+            device_id_type=MESH,
+        )
+
+    for copy in (plain_up[0], plain_down[0], sum_up[0], sum_down[0]):
+        copy.wait_recv()
+    def z_half(h):
+        total = x_own[h] + r_up[h] + r_down[h]
+        turned = jnp.transpose(total[:128, :])
+        rest = total[128:F, :]
+        for to in ((0, 1), (3, 2))[h]:
+            z_send[to, :64, :] = turned[64 * (to % 2) : 64 * (to % 2) + 64, :]
+            z_send[to, 64:72, :] = jnp.where(half == to % 2, rest, counted)
+
+            @pl.when(z != to)
+            def _():
+                z_copy(to).start()
+
+    z_half(0)
+    for copy in (plain_up[1], plain_down[1], sum_up[1], sum_down[1]):
+        copy.wait_recv()
+    z_half(1)
 
     w_copy.wait()
     for r in range(ROWS):
@@ -168,35 +240,18 @@
             )
             fg_ref[r, :, p : p + n] = (product * v16[:, p : p + n]).astype(BF16)
 
-    for copy in x_copies:
-        copy.wait_recv()
-    total = x_send[0] + x_recv[0] + x_recv[1] + x_recv[2]
-    turned = jnp.transpose(total[:128, :])
-    rest = total[128:F, :]
-    counted = c_send[...] + c_recv[0] + c_recv[1] + c_recv[2]
-    counted = counted + pltpu.roll(counted, 64, 1)
-    half = iota((8, 128), 1) // 64
-    for to in range(4):
-        z_send[to, :64, :] = turned[64 * to : 64 * to + 64, :]
-        tile = rest[:, 128 * (to // 2) : 128 * (to // 2) + 128]
-        z_send[to, 64:72, :] = jnp.where(half == to % 2, tile, counted)
-
-    z_copies = []
-    for d in (2, 1, 3):
-        to = (z + d) % 4
-        copy = pltpu.make_async_remote_copy(
-            src_ref=z_send.at[to],
-            dst_ref=z_recv.at[d - 1],
-            send_sem=z_ssem.at[d - 1],
-            recv_sem=z_rsem.at[d - 1],
-            device_id={"z": to},
-            device_id_type=MESH,
-        )
-        copy.start()
-        z_copies.append(copy)
-    for copy in z_copies:
-        copy.wait_recv()
-    nearer = z_send[z] + z_recv[0] + z_recv[1] + z_recv[2]
+    nearer = z_send[z]
+    for d in range(1, 4):
+        source = (z + d) % 4
+        pltpu.make_async_remote_copy(
+            src_ref=z_send.at[source],
+            dst_ref=z_recv.at[source],
+            send_sem=z_ssem.at[source],
+            recv_sem=z_rsem.at[source],
+            device_id={"z": source},
+            device_id_type=MESH,
+        ).wait_recv()
+        nearer = nearer + z_recv[source]
     for to in range(8):
         y_send[to, :8, :] = nearer[8 * to : 8 * to + 8, :]
         y_send[to, 8:16, :] = nearer[64:72, :]
@@ -227,8 +282,14 @@
     moved = pltpu.roll(tile, (128 - ((z % 2) * 64 + y * 8)) % 128, 1)
     wg_ref[:, 128:136] = jnp.transpose(moved)[:8, :] * scale
 
-    for copy in [to_far, to_mate, relay] + x_copies + z_copies + y_copies:
+    x_copies = first_up + first_down + plain_up + plain_down + sum_up + sum_down
+    for copy in [to_far, to_mate, relay] + x_copies + c_copies + y_copies:
         copy.wait_send()
+    for to in range(4):
+
+        @pl.when(z != to)
+        def _():
+            z_copy(to).wait_send()
 
 
 def local(field, cotangent, weight, lon_counts, point_mask):
@@ -250,17 +311,23 @@
             pltpu.VMEM((4, PART, WIDTH), BF16),
             pltpu.VMEM((ROWS, 8, LANES), F32),
             pltpu.VMEM((ROWS, F, PATCHES), BF16),
-            pltpu.VMEM((4, F, 256), F32),
-            pltpu.VMEM((3, F, 256), F32),
+            pltpu.VMEM((2, F, 128), F32),
+            pltpu.VMEM((2, F, 128), F32),
+            pltpu.VMEM((2, F, 128), F32),
+            pltpu.VMEM((2, F, 128), F32),
+            pltpu.VMEM((2, TOP, 128), F32),
+            pltpu.VMEM((2, F - TOP, 128), F32),
+            pltpu.VMEM((2, F, 128), F32),
+            pltpu.VMEM((2, F, 128), F32),
             pltpu.VMEM((8, 128), F32),
             pltpu.VMEM((3, 8, 128), F32),
             pltpu.VMEM((4, Z_ROWS, 128), F32),
-            pltpu.VMEM((3, Z_ROWS, 128), F32),
+            pltpu.VMEM((4, Z_ROWS, 128), F32),
             pltpu.VMEM((8, 16, 128), F32),
             pltpu.VMEM((7, 16, 128), F32),
             dma((ROWS,)), dma((ROWS,)), dma, dma, dma,
-            dma((3,)), dma((3,)), dma((3,)), dma((3,)), dma((3,)), dma((3,)),
-            dma((3,)), dma((3,)), dma((7,)), dma((7,)),
+            dma((3,)), dma((3,)), dma((6,)), dma((6,)), dma((6,)), dma((6,)), dma((3,)), dma((3,)),
+            dma((4,)), dma((4,)), dma((7,)), dma((7,)),
         ],
         compiler_params=pltpu.CompilerParams(
             collective_id=0, has_side_effects=True, vmem_limit_bytes=40 * 1024 * 1024

time: 42.2 us -> 39.5 us (0.936)
  the two profiles are of different devices: /device:TPU:1 before, /device:TPU:128 now
where the time goes in v3:
time: 39.5 us; the launch traced here: 39.4 us
  Pallas kernels  37.2 us (94%)
  local copies, waits for them, and re-layouts  1.56 us (4%)
  between operations  0.64 us (2%)
    pallas_call x1, Pallas kernels, local(): pl.pallas_call(kernel, out_shape=(pltpu.VMEM((ROWS, F, PATCHES), BF16), p...  37.2 us
    unnamed x2, local copies, waits for them, and re-layouts  1.56 us

profile of v3, /device:TPU:128, one launch (start us, length us, event | category | flops | bytes accessed | tf_op | source)
XLA Modules:
  0.0 39.4 jit_solution(12707002055152409013)
XLA Ops:
  0.6 37.2 %backward.1 = (bf16[5,136,642]{2,1,0:T(8,128)(2,1)S(1)}, f32[8,136]{1,0:T(8,128)S(1)}) custom-call(bf16[5,136,642]{2,1,0:T(8,128)(2,1)} %bitcast.3, bf16[5,642,1024]{2,1,0:T(8,128)(2,1)} %cot_hbm.1, bf16[136,1024]{1,0:T(8,128)(2,1)} %w_hbm.1, s32[5]{0:T(128)} %counts_hbm.1, s32[5,1284]{1,0:T(8,128)} %mask_hbm.1), custom_call_target="tpu_custom_call" | custom-call | tf_op jit(solution)/shard_map/backward/pallas_call | solution.py:300
  37.8 1.0 %copy.9 = bf16[5,642,136]{1,2,0:T(8,128)(2,1)} copy(bf16[5,642,136]{1,2,0:T(8,128)(2,1)S(1)} %bitcast.2) | data formatting | bytes 1746240
  38.8 0.6 %copy.10 = f32[8,136]{1,0:T(8,128)} copy(f32[8,136]{1,0:T(8,128)S(1)} %get-tuple-element.7) | data formatting | bytes 8704

commit v4 on v3

v4 whole, which is shorter than its diff:
```python
import functools

import jax
import jax.numpy as jnp
from jax import lax
from jax.experimental import pallas as pl
from jax.experimental.pallas import tpu as pltpu
from jax.sharding import Mesh
from jax.sharding import PartitionSpec as P

MESH = pl.DeviceIdType.MESH
AXES = ("x", "z", "y", "zh", "core")
LAT = ("x", "z", "y")
CHAN = ("zh", "core")
F32 = jnp.float32
BF16 = jnp.bfloat16

ROWS = 5
PATCHES = 642
F = 136
E = 1024
PART = 1284
WIDTH = 384
LANES = 768
Z_ROWS = 9
Y_ROWS = 18
TOP = 72


def iota(shape, dim):
    return lax.broadcasted_iota(jnp.int32, shape, dim)


def kernel(
    ft_hbm, cot_hbm, w_hbm, counts_hbm, mask_hbm,
    fg_ref, wg_ref,
    ft, cot, w, counts, masks, pick, valid, fm,
    x_all, x_own, s_up, s_down, r_all, c_send, c_recv, z_send, z_recv, y_send, y_recv,
    cot_sem, ft_sem, w_sem, counts_sem, mask_sem,
    m_ssem, m_rsem, x_ssem, x_rsem, c_ssem, c_rsem, z_ssem, z_rsem, y_ssem, y_rsem, heard,
):
    x, z, y = (lax.axis_index(a) for a in LAT)
    zh, core = (lax.axis_index(a) for a in CHAN)
    me = zh * 2 + core
    mate = zh * 2 + 1 - core
    far = (1 - zh) * 2 + core
    far_mate = (1 - zh) * 2 + 1 - core

    own_mask = pltpu.make_async_copy(mask_hbm, masks.at[me], mask_sem)
    own_mask.start()
    own_counts = pltpu.make_async_copy(counts_hbm, counts, counts_sem)
    own_counts.start()

    barrier = pltpu.get_barrier_semaphore()

    def greet(device):
        pl.semaphore_signal(barrier, inc=1, device_id=device, device_id_type=MESH)

    def neighbours(signal, axes):
        for axis, at, size in axes:
            signal({axis: (at + 1) % size})
            signal({axis: (at + size - 1) % size})

        @pl.when(z > 0)
        def _():
            signal({"z": z - 1})

        @pl.when(z < 3)
        def _():
            signal({"z": z + 1})

    beside = (z + 3) // 4 + (6 - z) // 4
    greet({"zh": 1 - zh})
    greet({"core": 1 - core})
    neighbours(greet, (("x", x, 4), ("y", y, 8)))

    def hear(i):
        def tell(device):
            pl.semaphore_signal(heard.at[i], inc=1, device_id=device, device_id_type=MESH)

        if i < 2:
            neighbours(tell, (("x", x, 4), ("y", y, 8))[1 - (i == 0) :])
        else:
            tell({"y": (y + 1) % 8})
            tell({"y": (y + 7) % 8})

    shards = (me, mate, far, far_mate)

    def fill(i):
        at = ((iota((PART, WIDTH), 0) + PART * shards[i]) >> 3) - 128 * shards[i]
        hit = at == iota((PART, WIDTH), 1)
        pick[i] = jnp.where(hit, 1.0, 0.0).astype(BF16)

    for i in range(4):
        fill(i)
    valid[...] = jnp.zeros_like(valid)

    own_mask.wait()
    own_counts.wait()
    w_copy = pltpu.make_async_copy(w_hbm, w, w_sem)
    cot_copies = [pltpu.make_async_copy(cot_hbm, cot, cot_sem)]
    ft_copies = [pltpu.make_async_copy(ft_hbm, ft, ft_sem)]

    def mask_to(i, shard, device):
        return pltpu.make_async_remote_copy(
            src_ref=masks.at[shard],
            dst_ref=masks.at[shard],
            send_sem=m_ssem,
            recv_sem=m_rsem.at[i],
            device_id=device,
            device_id_type=MESH,
        )

    def place(i):
        j = shards[i]
        spot = iota((8, PART), 1) + PART * j
        phase = (spot & 7) == iota((8, PART), 0)
        rows = []
        for r in range(ROWS):
            keep = jnp.logical_and(phase, spot < counts[r])
            line = jnp.broadcast_to(masks[j, r : r + 1, :], (8, PART)).astype(F32)
            rows.append(jnp.where(keep, line, 0.0))
        spread = jnp.concatenate(rows, axis=0).astype(BF16)
        placed = jnp.dot(spread, pick[i], preferred_element_type=F32)
        lanes = pl.ds(pl.multiple_of(j * 128, 128), WIDTH)
        for r in range(ROWS):
            valid[r, :, lanes] += placed[8 * r : 8 * r + 8]

    for c in ft_copies + cot_copies + [w_copy]:
        c.start()
    pl.semaphore_wait(barrier, 6 + beside)
    to_far = mask_to(0, me, {"zh": 1 - zh})
    to_far.start()
    to_mate = mask_to(1, me, {"core": 1 - core})
    to_mate.start()
    hear(0)
    place(0)
    to_mate.wait_recv()
    place(1)
    to_far.wait_recv()
    relay = mask_to(2, far, {"core": 1 - core})
    relay.start()
    place(2)
    for c in ft_copies:
        c.wait()
    relay.wait_recv()
    place(3)

    count = jnp.zeros((8, 128), F32)
    for r in range(ROWS):
        v = valid[r]
        for t in range(LANES // 128):
            count = count + v[:, 128 * t : 128 * t + 128]
        v = v[:, :PATCHES]
        v16 = jnp.concatenate([v, v], axis=0).astype(BF16)
        for c in range(0, 128, 16):
            fm[r, c : c + 16, :] = ft[r, c : c + 16, :] * v16
        fm[r, 128:136, :] = ft[r, 128:136, :] * v16[:8]
    c_send[...] = count
    for c in cot_copies:
        c.wait()

    top, low = pl.ds(0, TOP), pl.ds(TOP, F - TOP)
    up, down = (x + 1) % 4, (x + 3) % 4

    def block(to, ref):
        lanes = pl.ds(pl.multiple_of(to * 256, 256), 256)
        acc = jnp.dot(fm[0], cot[0, :, lanes], preferred_element_type=F32)
        for r in range(1, ROWS):
            acc = acc + jnp.dot(fm[r], cot[r, :, lanes], preferred_element_type=F32)
        ref[0] = acc[:, :128]
        ref[1] = acc[:, 128:]

    def x_copy(source, target, sem, to):
        return pltpu.make_async_remote_copy(
            src_ref=source,
            dst_ref=target,
            send_sem=x_ssem,
            recv_sem=sem,
            device_id={"x": to},
            device_id_type=MESH,
        )

    def joint(source, target, ssem, rsem, device):
        return pltpu.make_async_remote_copy(
            src_ref=source, dst_ref=target, send_sem=ssem, recv_sem=rsem, device_id=device, device_id_type=MESH
        )

    x_two, x_up, x_down = (x_all.at[i] for i in range(3))
    both = range(2)
    first_up = [x_copy(x_all.at[0, h, top], s_up.at[h], x_rsem.at[h], up) for h in both]
    first_down = [x_copy(x_all.at[0, h, low], s_down.at[h], x_rsem.at[2 + h], down) for h in both]
    plain_up = [x_copy(x_all.at[1, h, low], r_all.at[h, 0, low], x_rsem.at[4 + h], up) for h in both]
    plain_down = [x_copy(x_all.at[2, h, top], r_all.at[h, 1, top], x_rsem.at[4 + h], down) for h in both]
    sum_up = [x_copy(x_all.at[1, h, top], r_all.at[h, 0, top], x_rsem.at[4 + h], up) for h in both]
    sum_down = [x_copy(x_all.at[2, h, low], r_all.at[h, 1, low], x_rsem.at[4 + h], down) for h in both]
    x_in = [x_copy(r_all.at[h], r_all.at[h], x_rsem.at[4 + h], up) for h in both]

    block((x + 2) % 4, x_two)
    for h in range(2):
        first_up[h].start()
        first_down[h].start()
    pl.semaphore_wait(heard.at[0], 4 + beside)
    hear(1)
    for d in (2, 1, 3):
        copy = pltpu.make_async_remote_copy(
            src_ref=c_send,
            dst_ref=c_recv.at[d - 1],
            send_sem=c_ssem,
            recv_sem=c_rsem,
            device_id={"x": (x + d) % 4},
            device_id_type=MESH,
        )
        copy.start()
    block(up, x_up)
    plain_up[0].start()
    block(down, x_down)
    plain_down[0].start()
    block(x, x_own)
    pl.semaphore_wait(heard.at[1], 2 + beside)
    hear(2)
    for h in range(2):
        first_up[h].wait_recv()
        x_up[h, top, :] += s_up[h]
        sum_up[h].start()
        first_down[h].wait_recv()
        x_down[h, low, :] += s_down[h]
        sum_down[h].start()
        if h == 0:
            plain_up[1].start()
            plain_down[1].start()
    joint(c_recv, c_recv, c_ssem, c_rsem, {"x": up}).wait_recv()
    counted = c_send[...] + c_recv[0] + c_recv[1] + c_recv[2]
    counted = jnp.sum(counted, axis=0, keepdims=True)
    counted = counted + pltpu.roll(counted, 64, 1)
    half = iota((1, 128), 1) // 64

    def y_copy(h, d):
        to = (y + d) % 8
        return pltpu.make_async_remote_copy(
            src_ref=y_send.at[h, to],
            dst_ref=y_recv.at[h, d - 1],
            send_sem=y_ssem,
            recv_sem=y_rsem.at[h],
            device_id={"y": to},
            device_id_type=MESH,
        )

    def z_copy(to):
        return pltpu.make_async_remote_copy(
            src_ref=z_send.at[to],
            dst_ref=z_recv.at[(z - to + 3) % 4],
            send_sem=z_ssem,
            recv_sem=z_rsem,
            device_id={"z": to},
            device_id_type=MESH,
        )

    def y_half(h):
        total = x_own[h] + r_all[h, 0] + r_all[h, 1]
        turned = jnp.transpose(total[:128, :])
        rest = jnp.transpose(jnp.concatenate([total[128:F, :], jnp.zeros((120, 128), F32)], axis=0))
        for to in range(8):
            lines = jnp.zeros((8, 128), F32)
            for i in range(2):
                at = 64 * i + 8 * to
                y_send[h, to, 8 * i : 8 * i + 8, :] = turned[at : at + 8, :]
                lines = lines + pltpu.roll(rest[at : at + 8, :], 64 * i, 1, stride=8, stride_axis=0)
            y_send[h, to, 16:17, :] = jnp.sum(lines, axis=0, keepdims=True)
            y_send[h, to, 17:18, :] = counted
        for d in (4, 3, 5, 2, 6, 1, 7):
            y_copy(h, d).start()

    def z_half(h):
        joint(y_recv.at[h], y_recv.at[h], y_ssem, y_rsem.at[h], {"y": (y + 1) % 8}).wait_recv()
        near = y_send[h, y]
        for d in range(7):
            near = near + y_recv[h, d]
        for i in range(2):
            to = 2 * h + (i if h == 0 else 1 - i)
            z_send[to, :8, :] = near[8 * (to % 2) : 8 * (to % 2) + 8, :]
            z_send[to, 8:9, :] = jnp.where(half == to % 2, near[16:17, :], near[17:18, :])

            @pl.when(z != to)
            def _():
                z_copy(to).start()

    x_in[0].wait_recv()
    pl.semaphore_wait(heard.at[2], 2)
    y_half(0)
    x_in[1].wait_recv()
    y_half(1)

    w_copy.wait()
    for r in range(ROWS):
        v = valid[r][:, :PATCHES]
        v16 = jnp.concatenate([v] * 17, axis=0)
        for p in range(0, PATCHES, 256):
            n = min(256, PATCHES - p)
            product = lax.dot_general(
                w[...], cot[r, p : p + n, :], (((1,), (1,)), ((), ())), preferred_element_type=F32
            )
            fg_ref[r, :, p : p + n] = (product * v16[:, p : p + n]).astype(BF16)

    z_half(0)
    z_half(1)
    joint(z_recv, z_recv, z_ssem, z_rsem, {"z": (z + 1) % 4}).wait_recv()
    last = z_send[z] + z_recv[0] + z_recv[1] + z_recv[2]
    row = last[8:9, :]
    mine = half == z % 2
    points = jnp.sum(jnp.where(mine, 0.0, row), axis=1, keepdims=True)
    scale = lax.rsqrt(jnp.maximum(points, 1.0))
    wg_ref[:, :128] = last[:8, :] * scale
    kept = jnp.logical_and(((iota((8, 128), 1) >> 3) & 7) == iota((8, 128), 0), iota((8, 128), 1) // 64 == z % 2)
    tail = jnp.where(kept, jnp.broadcast_to(row, (8, 128)), 0.0)
    for step in (64, 32, 16, 8):
        tail = tail + pltpu.roll(tail, step, 1)
    wg_ref[:, 128:136] = tail[:, :8] * scale

    mask_to(0, pl.ds(0, 3), {"zh": 1 - zh}).wait_send()
    x_copy(x_all, x_all, x_rsem.at[0], up).wait_send()
    joint(c_recv, c_recv, c_ssem, c_rsem, {"x": up}).wait_send()
    joint(z_recv, z_recv, z_ssem, z_rsem, {"z": (z + 1) % 4}).wait_send()
    joint(y_recv, y_recv, y_ssem, y_rsem.at[0], {"y": (y + 1) % 8}).wait_send()


def store(fg, wg, fg_hbm, wg_hbm, fg_sem, wg_sem):
    copies = [pltpu.make_async_copy(wg, wg_hbm, wg_sem), pltpu.make_async_copy(fg, fg_hbm, fg_sem)]
    for copy in copies:
        copy.start()
    for copy in copies:
        copy.wait()


def local(field, cotangent, weight, lon_counts, point_mask):
    ft = jnp.transpose(field, (0, 2, 1))
    hbm = pl.BlockSpec(memory_space=pltpu.HBM)
    vmem = pl.BlockSpec(memory_space=pltpu.VMEM)
    dma = pltpu.SemaphoreType.DMA
    fg, wg = pl.pallas_call(
        kernel,
        out_shape=(pltpu.VMEM((ROWS, F, PATCHES), BF16), pltpu.VMEM((8, F), F32)),
        in_specs=[hbm] * 5,
        out_specs=(vmem, vmem),
        scratch_shapes=[
            pltpu.VMEM((ROWS, F, PATCHES), BF16),
            pltpu.VMEM((ROWS, PATCHES, E), BF16),
            pltpu.VMEM((F, E), BF16),
            pltpu.SMEM((ROWS,), jnp.int32),
            pltpu.VMEM((4, ROWS, PART), jnp.int32),
            pltpu.VMEM((4, PART, WIDTH), BF16),
            pltpu.VMEM((ROWS, 8, LANES), F32),
            pltpu.VMEM((ROWS, F, PATCHES), BF16),
            pltpu.VMEM((3, 2, F, 128), F32),
            pltpu.VMEM((2, F, 128), F32),
            pltpu.VMEM((2, TOP, 128), F32),
            pltpu.VMEM((2, F - TOP, 128), F32),
            pltpu.VMEM((2, 2, F, 128), F32),
            pltpu.VMEM((8, 128), F32),
            pltpu.VMEM((3, 8, 128), F32),
            pltpu.VMEM((4, Z_ROWS, 128), F32),
            pltpu.VMEM((3, Z_ROWS, 128), F32),
            pltpu.VMEM((2, 8, Y_ROWS, 128), F32),
            pltpu.VMEM((2, 7, Y_ROWS, 128), F32),
            dma, dma, dma, dma, dma,
            dma, dma((3,)), dma, dma((6,)), dma, dma, dma, dma, dma, dma((2,)),
            pltpu.SemaphoreType.REGULAR((3,)),
        ],
        compiler_params=pltpu.CompilerParams(
            collective_id=0, has_side_effects=True, vmem_limit_bytes=40 * 1024 * 1024
        ),
        name="backward",
    )(*(pltpu.with_memory_space_constraint(v, pltpu.HBM) for v in (ft, cotangent, weight, lon_counts, point_mask)))
    fg, wg = pl.pallas_call(
        store,
        out_shape=(
            jax.ShapeDtypeStruct((ROWS, F, PATCHES), BF16),
            jax.ShapeDtypeStruct((8, F), F32),
        ),
        in_specs=[vmem] * 2,
        out_specs=(hbm, hbm),
        scratch_shapes=[dma, dma],
        name="store",
    )(*(pltpu.with_memory_space_constraint(v, pltpu.VMEM) for v in (fg, wg)))
    return jnp.transpose(fg, (0, 2, 1)), wg


def solution(mesh):
    split = Mesh(mesh.devices.reshape(4, 4, 8, 2, 2), AXES)
    in_specs = (P(LAT, None, CHAN), P(LAT, None, None), P(CHAN, None), P(LAT), P(LAT, CHAN))
    out_specs = (P(LAT, None, CHAN), P(LAT, CHAN))
    return jax.shard_map(local, mesh=split, in_specs=in_specs, out_specs=out_specs, check_vma=False)
```

time: 39.5 us -> 37 us (0.937)
  the two profiles are of different devices: /device:TPU:128 before, /device:TPU:1 now
where the time goes in v4:
time: 37 us; the launch traced here: 36.4 us
  Pallas kernels  35.7 us (96%)
  between operations  0.64 us (2%)
    pallas_call x1, Pallas kernels, local(): pl.pallas_call(kernel, out_shape=(pltpu.VMEM((ROWS, F, PATCHES), BF16), p...  34.7 us
    pallas_call x1, Pallas kernels, local(): pl.pallas_call(store, out_shape=(jax.ShapeDtypeStruct((ROWS, F, PATCHES),...  0.99 us

profile of v4, /device:TPU:1, one launch (start us, length us, event | category | flops | bytes accessed | tf_op | source)
XLA Modules:
  0.0 36.4 jit_solution(13641990767369022165)
XLA Ops:
  0.6 34.7 %backward.1 = (bf16[5,136,642]{2,1,0:T(8,128)(2,1)S(1)}, f32[8,136]{1,0:T(8,128)S(1)}) custom-call(bf16[5,136,642]{2,1,0:T(8,128)(2,1)} %bitcast.2, bf16[5,642,1024]{2,1,0:T(8,128)(2,1)} %cot_hbm.1, bf16[136,1024]{1,0:T(8,128)(2,1)} %w_hbm.1, s32[5]{0:T(128)} %counts_hbm.1, s32[5,1284]{1,0:T(8,128)} %mask_hbm.1), custom_call_target="tpu_custom_call" | custom-call | tf_op jit(solution)/shard_map/backward/pallas_call | solution.py:340
  35.4 1.0 %store.1 = (bf16[5,136,642]{2,1,0:T(8,128)(2,1)}, f32[8,136]{1,0:T(8,128)}) custom-call(bf16[5,136,642]{2,1,0:T(8,128)(2,1)S(1)} %get-tuple-element.6.fg, f32[8,136]{1,0:T(8,128)S(1)} %get-tuple-element.7.wg), custom_call_target="tpu_custom_call" | custom-call | tf_op jit(solution)/shard_map/store/pallas_call | solution.py:374
